TPU v7x, 32 devices: a whole 2x2x4 slice. The times are simulated.
32 devices in a mesh: grp: 2 (over x), tp: 4 (over y, core), pp: 4 (over z).
Axes of the slice: x: 2, y: 2, z: 4, core: 2. Of those that a mesh axis runs over, the one named last changes fastest.
Arguments:
- tokens: bfloat16 [1024, 8192], P('grp', 'tp'), parts along dimension 0, may hold values from -12 to 12
- gain: bfloat16 [4, 8192], P('pp', 'tp'), may hold values from 0.099609375 to 1.8984375
- q_weight: bfloat16 [4, 8192, 4096], P('pp', None, 'tp'), may hold values from -0.5 to 0.5
- kv_weight: bfloat16 [4, 8192, 2048], P('pp', None, 'tp'), may hold values from -0.5 to 0.5
- out_weight: bfloat16 [4, 4096, 8192], P('pp', None, 'tp'), may hold values from -0.09375 to 0.09375
- page_table: int32 [4, 8, 128], P('pp'), may hold values from 0 to 1023, as said below
- segment_ids: int32 [1024], P('grp'), parts along dimension 0, may hold values from 0 to 2, never falling along the last dimension, each value on 1 to 256 neighbouring positions
Outputs:
- hidden: bfloat16 [1024, 8192], P(('grp', 'pp'), 'tp'), parts along dimension 0
- kv_cache: bfloat16 [4, 2048, 4, 256], P('pp', ('grp', 'tp')), parts along dimension 1
There are 2 independent parts, one for each index of `grp`. A program takes and returns all parts, laid end to end along the dimension named above; an argument that names none is the same for every part. Nothing has to cross between parts.
Inputs may be any that keep to these rules, and one draw needn't show every extreme that they name: `page_table`: every entry of a layer's table is distinct and every one of the 1024 values occurs once. For each layer, head and micro-batch the 16 blocks form a run; in each run half of the devices receive exactly 8 pages and the others none, so each device receives exactly 256 pages of a layer.
All inputs are finite; a program needn't handle non-finite values.
Results may differ from a plain program's by a relative error of at most 0.017.
Values may be sent and summed in bfloat16 or wider, within the bound.
A program may use at most 128 MiB of HBM per device.

v0:
```python
import math
import jax
import jax.numpy as jnp
from jax import lax
from jax.sharding import PartitionSpec as P

MODEL_WIDTH = 8192
HEAD_SIZE = 128
KEY_VALUE_HEADS = 8
MB_TOK = 64
MICRO_BATCHES = 8
PAGE_TOKENS = 4
eps_norm = 1e-05


def partner_2(x, axis, apart):
    return lax.ppermute(x, axis, [(i, i ^ 1 << apart) for i in range(lax.axis_size(axis))])


def shifted(x, axis, by):
    peers = lax.axis_size(axis)
    pairs = [(i, i + by) for i in range(peers) if 0 <= i + by < peers]
    return lax.ppermute(x, axis, pairs)


def from_root(x, axis, root):
    mine = lax.axis_index(axis) == root
    return lax.psum(jnp.where(mine, x, jnp.zeros_like(x)), axis)


def send_pages(kv_own, page_rows, micro_idx, is_live, kv_cache, first_head, tensor_parallel_width):
    row_count = kv_own.shape[0]
    kv_cols = kv_own.shape[1]
    head_width = kv_cache.shape[2]
    cache_page_count = kv_cache.shape[0]
    held_heads = max(1, kv_cols // head_width)
    unit_cols = kv_cols // held_heads
    blocks = row_count // PAGE_TOKENS
    paged_rows = (
        kv_own.reshape(blocks, PAGE_TOKENS, held_heads, unit_cols)
        .transpose(2, 0, 1, 3)
        .reshape(held_heads * blocks, PAGE_TOKENS * unit_cols)
    )
    target_pages = lax.dynamic_slice(
        page_rows, (first_head, micro_idx * blocks), (held_heads, blocks)
    ).reshape(-1)
    device = target_pages // cache_page_count
    cache_page_index = target_pages % cache_page_count
    page_count = held_heads * blocks
    capacity = 2 * page_count // tensor_parallel_width
    onehot = (
        device[:, None] == jnp.arange(tensor_parallel_width, dtype=jnp.int32)[None, :]
    ).astype(jnp.int32)
    earlier = jnp.cumsum(onehot, axis=0) - onehot
    arrival = jnp.sum(earlier * onehot, axis=1)
    position = device * capacity + arrival
    outgoing = (
        jnp.zeros((tensor_parallel_width * capacity, PAGE_TOKENS * unit_cols), jnp.bfloat16)
        .at[position]
        .set(paged_rows)
    )
    labels = (
        jnp.full((tensor_parallel_width * capacity,), cache_page_count, jnp.int32)
        .at[position]
        .set(jnp.where(is_live, cache_page_index, cache_page_count))
    )
    incoming, landing = (
        lax.all_to_all(outgoing, "tp", split_axis=0, concat_axis=0, tiled=True),
        lax.all_to_all(labels, "tp", split_axis=0, concat_axis=0, tiled=True),
    )
    offsets = jnp.arange(tensor_parallel_width, dtype=jnp.int32) * kv_cols % head_width
    lane_ids = jnp.arange(head_width, dtype=jnp.int32)
    within = jnp.arange(unit_cols, dtype=jnp.int32)
    placer = (lane_ids[None, None, :] == offsets[:, None, None] + within[None, :, None]).astype(
        jnp.bfloat16
    )
    spread = jnp.einsum(
        "snw,swv->snv",
        incoming.reshape(tensor_parallel_width, capacity * PAGE_TOKENS, unit_cols),
        placer,
        preferred_element_type=jnp.float32,
    ).astype(jnp.bfloat16)
    return kv_cache.at[landing].add(
        spread.reshape(tensor_parallel_width * capacity, PAGE_TOKENS, head_width), mode="drop"
    )


def body(tokens, gain, q_weight, kv_weight, out_weight, page_table, segment_ids):
    tensor_parallel_width = lax.axis_size("tp")
    pp_size = lax.axis_size("pp")
    tp_rank = lax.axis_index("tp")
    section_idx = lax.axis_index("pp")
    w_query = q_weight[0]
    w_keyval = kv_weight[0]
    w_output = out_weight[0]
    page_rows = page_table[0]
    local_width = tokens.shape[1]
    row_total = tokens.shape[0]
    row_count = MB_TOK
    head_dim = HEAD_SIZE
    kv_cols = w_keyval.shape[1]
    held_heads = max(1, kv_cols // (2 * head_dim))
    q_heads = w_query.shape[1] // head_dim
    per_kv = q_heads // held_heads
    first_head = tp_rank * kv_cols // (2 * head_dim)
    cache_page_count = KEY_VALUE_HEADS * (row_total // PAGE_TOKENS) // tensor_parallel_width
    score_scale = 1.0 / math.sqrt(head_dim)
    step_count = MICRO_BATCHES + pp_size - 1
    key_pos = jnp.arange(row_total, dtype=jnp.int32)

    def add_columns(block_cols):
        return (
            jnp.dot(block_cols, w_query, preferred_element_type=jnp.float32),
            jnp.dot(block_cols, w_keyval, preferred_element_type=jnp.float32),
        )

    def add_outputs(block_cols):
        return jnp.dot(block_cols, w_output, preferred_element_type=jnp.float32)

    def one_step(step_idx, state_tuple):
        received, kv_buffer, kv_cache, collected = state_tuple
        micro_raw = step_idx - section_idx
        is_live = (micro_raw >= 0) & (micro_raw < MICRO_BATCHES)
        micro_idx = jnp.clip(micro_raw, 0, MICRO_BATCHES - 1)
        row_start = micro_idx * row_count
        first_rows = lax.dynamic_slice_in_dim(tokens, row_start, row_count, 0)
        current = jnp.where(section_idx == 0, first_rows, received)
        widened = current.astype(jnp.float32)
        partial_sq = jnp.sum(widened * widened, axis=1, keepdims=True)
        mean_sq = lax.psum(partial_sq, "tp") / MODEL_WIDTH
        normed = (widened * lax.rsqrt(mean_sq + eps_norm) * gain.astype(jnp.float32)).astype(
            jnp.bfloat16
        )
        query_sum, keyval_sum = add_columns(lax.all_gather(normed, "tp", axis=1, tiled=True))
        query_matrix = query_sum.astype(jnp.bfloat16)
        kv_own = keyval_sum.astype(jnp.bfloat16)
        if tensor_parallel_width > KEY_VALUE_HEADS:
            partner = partner_2(kv_own, "tp", 0)
            first_half = tp_rank % 2 == 0
            head_pair = jnp.where(
                first_half,
                jnp.concatenate([kv_own, partner], axis=1),
                jnp.concatenate([partner, kv_own], axis=1),
            )
        else:
            head_pair = kv_own
        kv_cache = send_pages(
            kv_own, page_rows, micro_idx, is_live, kv_cache, first_head, tensor_parallel_width
        )
        refreshed = lax.dynamic_update_slice_in_dim(kv_buffer, head_pair, row_start, 0)
        kv_buffer = jnp.where(is_live, refreshed, kv_buffer)
        kv_view = kv_buffer.reshape(row_total, held_heads, 2, head_dim)
        grouped_queries = query_matrix.reshape(row_count, held_heads, per_kv, head_dim)
        scores = (
            jnp.einsum(
                "qgpd,kgd->gpqk",
                grouped_queries,
                kv_view[:, :, 0],
                preferred_element_type=jnp.float32,
            )
            * score_scale
        )
        query_pos = row_start + jnp.arange(row_count, dtype=jnp.int32)
        seg_query = lax.dynamic_slice_in_dim(segment_ids, row_start, row_count, 0)
        allowed = (key_pos[None, :] <= query_pos[:, None]) & (
            segment_ids[None, :] == seg_query[:, None]
        )
        scores = jnp.where(allowed[None, None], scores, -1e30)
        row_max = jnp.max(scores, axis=-1, keepdims=True)
        raised = jnp.exp(scores - row_max)
        weights = (raised / jnp.sum(raised, axis=-1, keepdims=True)).astype(jnp.bfloat16)
        attended = jnp.einsum(
            "gpqk,kgd->qgpd", weights, kv_view[:, :, 1], preferred_element_type=jnp.float32
        )
        attended = attended.astype(jnp.bfloat16).reshape(row_count, q_heads * head_dim)
        projected = add_outputs(lax.all_gather(attended, "tp", axis=1, tiled=True))
        produced = (widened + projected).astype(jnp.bfloat16)
        placed = lax.dynamic_update_slice_in_dim(collected, produced, row_start, 0)
        collected = jnp.where(is_live & (section_idx == pp_size - 1), placed, collected)
        handed = shifted(produced, "pp", 1)
        return (handed, kv_buffer, kv_cache, collected)

    initial = (
        jnp.zeros((row_count, local_width), jnp.bfloat16),
        jnp.zeros((row_total, held_heads * 2 * head_dim), jnp.bfloat16),
        jnp.zeros((cache_page_count, PAGE_TOKENS, 2 * head_dim), jnp.bfloat16),
        jnp.zeros((row_total, local_width), jnp.bfloat16),
    )
    finished = lax.fori_loop(0, step_count, one_step, initial)
    whole_final = from_root(finished[3], "pp", pp_size - 1)
    share_rows = row_total // pp_size
    hidden = lax.dynamic_slice_in_dim(whole_final, section_idx * share_rows, share_rows, 0)
    return (hidden, finished[2][None])


def solution(mesh):
    placed = (
        P("grp", "tp"),
        P("pp", "tp"),
        P("pp", None, "tp"),
        P("pp", None, "tp"),
        P("pp", None, "tp"),
        P("pp", None, None),
        P("grp"),
    )
    return jax.shard_map(
        body,
        mesh=mesh,
        in_specs=placed,
        out_specs=(P(("grp", "pp"), "tp"), P("pp", ("grp", "tp"), None, None)),
        check_vma=False,
    )
```

profile of v0, /device:TPU:0, one launch (start us, length us, event | category | flops | bytes accessed | tf_op | source)
XLA Modules:
  0.0 928.2 jit_solution(15119671289388943089)
XLA Ops:
  9.8 821.5 %while.22 = (s32[]{:T(128)}, bf16[64,2048]{1,0:T(8,128)(2,1)S(1)}, bf16[512,512]{1,0:T(8,128)(2,1)S(1)}, bf16[256,4,256]{2,1,0:T(4,128)(2,1)S(1)}, bf16[512,2048...) while((s32[]{:T(128)}, bf16[64,2048]{1,0:T(8,128)(2,1)S(1)}, ...), condition=%wide.region_10.11_spmd.clone, body=%wide.region_0.10_spmd.clone.sunk | while | flops 2923866880 | bytes 66799608 | solution.py:189
  11.1 8.4 psum.24
  43.0 8.8 convolution_convert_fusion.6
  54.5 7.2 all_gather.25
  61.6 9.6 %select_dynamic-update-slice_fusion.2 = (bf16[512,2048]{1,0:T(8,128)(2,1)}, bf16[64,2048]{1,0:T(8,128)(2,1)S(1)}) fusion(bf16[512,2048]{1,0:T(8,128)(2,1)} %get-tuple-element.624, s32[]{:T(128)S(6)} %select_n.328, pred[]{:T(512)S(6)} %and.146, bf16[64,4096]{1,0:T(8,128)(2,1)S(1)} %all_gather.25, bf16[4096,2048]{1,0:T(8,128)(2,1)} %get-tuple-element.658, ...), kind=kOutput, calls=%fused_computation.27.clone.1 | convolution fusion | flops 1074266112 | bytes 18350084 | tf_op jit(solution)/shard_map/while/body/eval_jaxpr/dot_general | solution.py:118
  117.3 8.8 convolution_convert_fusion.6
  136.3 9.5 %select_dynamic-update-slice_fusion.2 = (bf16[512,2048]{1,0:T(8,128)(2,1)}, bf16[64,2048]{1,0:T(8,128)(2,1)S(1)}) fusion(bf16[512,2048]{1,0:T(8,128)(2,1)} %get-tuple-element.624, s32[]{:T(128)S(6)} %select_n.328, pred[]{:T(512)S(6)} %and.146, bf16[64,4096]{1,0:T(8,128)(2,1)S(1)} %all_gather.25, bf16[4096,2048]{1,0:T(8,128)(2,1)} %get-tuple-element.658, ...), kind=kOutput, calls=%fused_computation.27.clone.1 | convolution fusion | flops 1074266112 | bytes 18350084 | tf_op jit(solution)/shard_map/while/body/eval_jaxpr/dot_general | solution.py:118
  191.6 8.8 convolution_convert_fusion.6
  203.0 7.2 all_gather.25
  210.2 9.5 %select_dynamic-update-slice_fusion.2 = (bf16[512,2048]{1,0:T(8,128)(2,1)}, bf16[64,2048]{1,0:T(8,128)(2,1)S(1)}) fusion(bf16[512,2048]{1,0:T(8,128)(2,1)} %get-tuple-element.624, s32[]{:T(128)S(6)} %select_n.328, pred[]{:T(512)S(6)} %and.146, bf16[64,4096]{1,0:T(8,128)(2,1)S(1)} %all_gather.25, bf16[4096,2048]{1,0:T(8,128)(2,1)} %get-tuple-element.658, ...), kind=kOutput, calls=%fused_computation.27.clone.1 | convolution fusion | flops 1074266112 | bytes 18350084 | tf_op jit(solution)/shard_map/while/body/eval_jaxpr/dot_general | solution.py:118
  265.8 8.8 convolution_convert_fusion.6
  284.8 9.5 %select_dynamic-update-slice_fusion.2 = (bf16[512,2048]{1,0:T(8,128)(2,1)}, bf16[64,2048]{1,0:T(8,128)(2,1)S(1)}) fusion(bf16[512,2048]{1,0:T(8,128)(2,1)} %get-tuple-element.624, s32[]{:T(128)S(6)} %select_n.328, pred[]{:T(512)S(6)} %and.146, bf16[64,4096]{1,0:T(8,128)(2,1)S(1)} %all_gather.25, bf16[4096,2048]{1,0:T(8,128)(2,1)} %get-tuple-element.658, ...), kind=kOutput, calls=%fused_computation.27.clone.1 | convolution fusion | flops 1074266112 | bytes 18350084 | tf_op jit(solution)/shard_map/while/body/eval_jaxpr/dot_general | solution.py:118
  340.0 8.8 convolution_convert_fusion.6
  351.5 7.2 all_gather.25
  358.6 9.5 %select_dynamic-update-slice_fusion.2 = (bf16[512,2048]{1,0:T(8,128)(2,1)}, bf16[64,2048]{1,0:T(8,128)(2,1)S(1)}) fusion(bf16[512,2048]{1,0:T(8,128)(2,1)} %get-tuple-element.624, s32[]{:T(128)S(6)} %select_n.328, pred[]{:T(512)S(6)} %and.146, bf16[64,4096]{1,0:T(8,128)(2,1)S(1)} %all_gather.25, bf16[4096,2048]{1,0:T(8,128)(2,1)} %get-tuple-element.658, ...), kind=kOutput, calls=%fused_computation.27.clone.1 | convolution fusion | flops 1074266112 | bytes 18350084 | tf_op jit(solution)/shard_map/while/body/eval_jaxpr/dot_general | solution.py:118
  414.7 8.8 convolution_convert_fusion.6
  426.5 7.2 all_gather.25
  433.7 9.5 %select_dynamic-update-slice_fusion.2 = (bf16[512,2048]{1,0:T(8,128)(2,1)}, bf16[64,2048]{1,0:T(8,128)(2,1)S(1)}) fusion(bf16[512,2048]{1,0:T(8,128)(2,1)} %get-tuple-element.624, s32[]{:T(128)S(6)} %select_n.328, pred[]{:T(512)S(6)} %and.146, bf16[64,4096]{1,0:T(8,128)(2,1)S(1)} %all_gather.25, bf16[4096,2048]{1,0:T(8,128)(2,1)} %get-tuple-element.658, ...), kind=kOutput, calls=%fused_computation.27.clone.1 | convolution fusion | flops 1074266112 | bytes 18350084 | tf_op jit(solution)/shard_map/while/body/eval_jaxpr/dot_general | solution.py:118
  488.9 8.8 convolution_convert_fusion.6
  500.2 7.2 all_gather.25
  507.4 9.5 %select_dynamic-update-slice_fusion.2 = (bf16[512,2048]{1,0:T(8,128)(2,1)}, bf16[64,2048]{1,0:T(8,128)(2,1)S(1)}) fusion(bf16[512,2048]{1,0:T(8,128)(2,1)} %get-tuple-element.624, s32[]{:T(128)S(6)} %select_n.328, pred[]{:T(512)S(6)} %and.146, bf16[64,4096]{1,0:T(8,128)(2,1)S(1)} %all_gather.25, bf16[4096,2048]{1,0:T(8,128)(2,1)} %get-tuple-element.658, ...), kind=kOutput, calls=%fused_computation.27.clone.1 | convolution fusion | flops 1074266112 | bytes 18350084 | tf_op jit(solution)/shard_map/while/body/eval_jaxpr/dot_general | solution.py:118
  563.5 8.8 convolution_convert_fusion.6
  582.4 9.5 %select_dynamic-update-slice_fusion.2 = (bf16[512,2048]{1,0:T(8,128)(2,1)}, bf16[64,2048]{1,0:T(8,128)(2,1)S(1)}) fusion(bf16[512,2048]{1,0:T(8,128)(2,1)} %get-tuple-element.624, s32[]{:T(128)S(6)} %select_n.328, pred[]{:T(512)S(6)} %and.146, bf16[64,4096]{1,0:T(8,128)(2,1)S(1)} %all_gather.25, bf16[4096,2048]{1,0:T(8,128)(2,1)} %get-tuple-element.658, ...), kind=kOutput, calls=%fused_computation.27.clone.1 | convolution fusion | flops 1074266112 | bytes 18350084 | tf_op jit(solution)/shard_map/while/body/eval_jaxpr/dot_general | solution.py:118
  637.7 8.8 convolution_convert_fusion.6
  649.5 7.2 all_gather.25
  656.6 9.5 %select_dynamic-update-slice_fusion.2 = (bf16[512,2048]{1,0:T(8,128)(2,1)}, bf16[64,2048]{1,0:T(8,128)(2,1)S(1)}) fusion(bf16[512,2048]{1,0:T(8,128)(2,1)} %get-tuple-element.624, s32[]{:T(128)S(6)} %select_n.328, pred[]{:T(512)S(6)} %and.146, bf16[64,4096]{1,0:T(8,128)(2,1)S(1)} %all_gather.25, bf16[4096,2048]{1,0:T(8,128)(2,1)} %get-tuple-element.658, ...), kind=kOutput, calls=%fused_computation.27.clone.1 | convolution fusion | flops 1074266112 | bytes 18350084 | tf_op jit(solution)/shard_map/while/body/eval_jaxpr/dot_general | solution.py:118
  712.3 8.8 convolution_convert_fusion.6
  731.2 9.5 %select_dynamic-update-slice_fusion.2 = (bf16[512,2048]{1,0:T(8,128)(2,1)}, bf16[64,2048]{1,0:T(8,128)(2,1)S(1)}) fusion(bf16[512,2048]{1,0:T(8,128)(2,1)} %get-tuple-element.624, s32[]{:T(128)S(6)} %select_n.328, pred[]{:T(512)S(6)} %and.146, bf16[64,4096]{1,0:T(8,128)(2,1)S(1)} %all_gather.25, bf16[4096,2048]{1,0:T(8,128)(2,1)} %get-tuple-element.658, ...), kind=kOutput, calls=%fused_computation.27.clone.1 | convolution fusion | flops 1074266112 | bytes 18350084 | tf_op jit(solution)/shard_map/while/body/eval_jaxpr/dot_general | solution.py:118
  786.4 8.8 convolution_convert_fusion.6
  798.2 7.2 all_gather.25
  805.4 9.5 %select_dynamic-update-slice_fusion.2 = (bf16[512,2048]{1,0:T(8,128)(2,1)}, bf16[64,2048]{1,0:T(8,128)(2,1)S(1)}) fusion(bf16[512,2048]{1,0:T(8,128)(2,1)} %get-tuple-element.624, s32[]{:T(128)S(6)} %select_n.328, pred[]{:T(512)S(6)} %and.146, bf16[64,4096]{1,0:T(8,128)(2,1)S(1)} %all_gather.25, bf16[4096,2048]{1,0:T(8,128)(2,1)} %get-tuple-element.658, ...), kind=kOutput, calls=%fused_computation.27.clone.1 | convolution fusion | flops 1074266112 | bytes 18350084 | tf_op jit(solution)/shard_map/while/body/eval_jaxpr/dot_general | solution.py:118
  832.9 86.3 %all-reduce.2.cloned.1.call-done = bf16[512,2048]{1,0:T(8,128)(2,1)} async-done(((bf16[512,2048]{1,0:T(8,128)(2,1)}), bf16[512,2048]{1,0:T(8,128)(2,1)}) %all-reduce.2.cloned.1.call-update) | async-done | bytes 2097168 | tf_op jit(solution)/shard_map/psum | solution.py:28
  (611 shorter events, 563.7 us)
Async XLA Ops:
  9.8 27.7 %all-gather.2.cloned.1.call-start = ((), (), s32[]{:S(2)}) async-start(), calls=%async_computation.3 | async-start | bytes 1310720 | tf_op jit(solution)/shard_map/while/body/eval_jaxpr/all_gather | solution.py:134
  71.2 16.3 %collective-permute-start = (bf16[64,2048]{1,0:T(8,128)(2,1)S(1)}, bf16[64,2048]{1,0:T(8,128)(2,1)S(1)}, u32[]{:S(2)}, u32[]{:S(2)}) collective-permute-start(bf16[64,2048]{1,0:T(8,128)(2,1)S(1)} %get-tuple-element.589), channel_id=1, source_target_pairs={{0,1},{1,2},{2,3},{4,5},{5,6},{6,7},{8,9},{9,10},{10,11},{12,13},{... | collective-permute-start | bytes 786440 | tf_op jit(solution)/shard_map/while/body/eval_jaxpr/ppermute | solution.py:23
  76.0 7.9 all-to-all-start.1
  87.5 24.3 %all-gather.2.cloned.1.call-start = ((), (), s32[]{:S(2)}) async-start(), calls=%async_computation.3 | async-start | bytes 1310720 | tf_op jit(solution)/shard_map/while/body/eval_jaxpr/all_gather | solution.py:134
  145.9 15.9 %collective-permute-start = (bf16[64,2048]{1,0:T(8,128)(2,1)S(1)}, bf16[64,2048]{1,0:T(8,128)(2,1)S(1)}, u32[]{:S(2)}, u32[]{:S(2)}) collective-permute-start(bf16[64,2048]{1,0:T(8,128)(2,1)S(1)} %get-tuple-element.589), channel_id=1, source_target_pairs={{0,1},{1,2},{2,3},{4,5},{5,6},{6,7},{8,9},{9,10},{10,11},{12,13},{... | collective-permute-start | bytes 786440 | tf_op jit(solution)/shard_map/while/body/eval_jaxpr/ppermute | solution.py:23
  150.3 7.9 all-to-all-start.1
  161.8 24.3 %all-gather.2.cloned.1.call-start = ((), (), s32[]{:S(2)}) async-start(), calls=%async_computation.3 | async-start | bytes 1310720 | tf_op jit(solution)/shard_map/while/body/eval_jaxpr/all_gather | solution.py:134
  219.7 16.7 %collective-permute-start = (bf16[64,2048]{1,0:T(8,128)(2,1)S(1)}, bf16[64,2048]{1,0:T(8,128)(2,1)S(1)}, u32[]{:S(2)}, u32[]{:S(2)}) collective-permute-start(bf16[64,2048]{1,0:T(8,128)(2,1)S(1)} %get-tuple-element.589), channel_id=1, source_target_pairs={{0,1},{1,2},{2,3},{4,5},{5,6},{6,7},{8,9},{9,10},{10,11},{12,13},{... | collective-permute-start | bytes 786440 | tf_op jit(solution)/shard_map/while/body/eval_jaxpr/ppermute | solution.py:23
  225.0 7.9 all-to-all-start.1
  236.5 23.8 %all-gather.2.cloned.1.call-start = ((), (), s32[]{:S(2)}) async-start(), calls=%async_computation.3 | async-start | bytes 1310720 | tf_op jit(solution)/shard_map/while/body/eval_jaxpr/all_gather | solution.py:134
  294.3 15.9 %collective-permute-start = (bf16[64,2048]{1,0:T(8,128)(2,1)S(1)}, bf16[64,2048]{1,0:T(8,128)(2,1)S(1)}, u32[]{:S(2)}, u32[]{:S(2)}) collective-permute-start(bf16[64,2048]{1,0:T(8,128)(2,1)S(1)} %get-tuple-element.589), channel_id=1, source_target_pairs={{0,1},{1,2},{2,3},{4,5},{5,6},{6,7},{8,9},{9,10},{10,11},{12,13},{... | collective-permute-start | bytes 786440 | tf_op jit(solution)/shard_map/while/body/eval_jaxpr/ppermute | solution.py:23
  298.8 7.9 all-to-all-start.1
  310.2 24.3 %all-gather.2.cloned.1.call-start = ((), (), s32[]{:S(2)}) async-start(), calls=%async_computation.3 | async-start | bytes 1310720 | tf_op jit(solution)/shard_map/while/body/eval_jaxpr/all_gather | solution.py:134
  368.2 16.7 %collective-permute-start = (bf16[64,2048]{1,0:T(8,128)(2,1)S(1)}, bf16[64,2048]{1,0:T(8,128)(2,1)S(1)}, u32[]{:S(2)}, u32[]{:S(2)}) collective-permute-start(bf16[64,2048]{1,0:T(8,128)(2,1)S(1)} %get-tuple-element.589), channel_id=1, source_target_pairs={{0,1},{1,2},{2,3},{4,5},{5,6},{6,7},{8,9},{9,10},{10,11},{12,13},{... | collective-permute-start | bytes 786440 | tf_op jit(solution)/shard_map/while/body/eval_jaxpr/ppermute | solution.py:23
  373.4 7.9 all-to-all-start.1
  384.9 24.3 %all-gather.2.cloned.1.call-start = ((), (), s32[]{:S(2)}) async-start(), calls=%async_computation.3 | async-start | bytes 1310720 | tf_op jit(solution)/shard_map/while/body/eval_jaxpr/all_gather | solution.py:134
  443.2 15.9 %collective-permute-start = (bf16[64,2048]{1,0:T(8,128)(2,1)S(1)}, bf16[64,2048]{1,0:T(8,128)(2,1)S(1)}, u32[]{:S(2)}, u32[]{:S(2)}) collective-permute-start(bf16[64,2048]{1,0:T(8,128)(2,1)S(1)} %get-tuple-element.589), channel_id=1, source_target_pairs={{0,1},{1,2},{2,3},{4,5},{5,6},{6,7},{8,9},{9,10},{10,11},{12,13},{... | collective-permute-start | bytes 786440 | tf_op jit(solution)/shard_map/while/body/eval_jaxpr/ppermute | solution.py:23
  447.7 7.9 all-to-all-start.1
  459.1 24.2 %all-gather.2.cloned.1.call-start = ((), (), s32[]{:S(2)}) async-start(), calls=%async_computation.3 | async-start | bytes 1310720 | tf_op jit(solution)/shard_map/while/body/eval_jaxpr/all_gather | solution.py:134
  516.9 16.8 %collective-permute-start = (bf16[64,2048]{1,0:T(8,128)(2,1)S(1)}, bf16[64,2048]{1,0:T(8,128)(2,1)S(1)}, u32[]{:S(2)}, u32[]{:S(2)}) collective-permute-start(bf16[64,2048]{1,0:T(8,128)(2,1)S(1)} %get-tuple-element.589), channel_id=1, source_target_pairs={{0,1},{1,2},{2,3},{4,5},{5,6},{6,7},{8,9},{9,10},{10,11},{12,13},{... | collective-permute-start | bytes 786440 | tf_op jit(solution)/shard_map/while/body/eval_jaxpr/ppermute | solution.py:23
  522.3 7.9 all-to-all-start.1
  533.7 24.2 %all-gather.2.cloned.1.call-start = ((), (), s32[]{:S(2)}) async-start(), calls=%async_computation.3 | async-start | bytes 1310720 | tf_op jit(solution)/shard_map/while/body/eval_jaxpr/all_gather | solution.py:134
  592.0 15.9 %collective-permute-start = (bf16[64,2048]{1,0:T(8,128)(2,1)S(1)}, bf16[64,2048]{1,0:T(8,128)(2,1)S(1)}, u32[]{:S(2)}, u32[]{:S(2)}) collective-permute-start(bf16[64,2048]{1,0:T(8,128)(2,1)S(1)} %get-tuple-element.589), channel_id=1, source_target_pairs={{0,1},{1,2},{2,3},{4,5},{5,6},{6,7},{8,9},{9,10},{10,11},{12,13},{... | collective-permute-start | bytes 786440 | tf_op jit(solution)/shard_map/while/body/eval_jaxpr/ppermute | solution.py:23
  596.4 7.9 all-to-all-start.1
  607.9 24.3 %all-gather.2.cloned.1.call-start = ((), (), s32[]{:S(2)}) async-start(), calls=%async_computation.3 | async-start | bytes 1310720 | tf_op jit(solution)/shard_map/while/body/eval_jaxpr/all_gather | solution.py:134
  666.2 16.4 %collective-permute-start = (bf16[64,2048]{1,0:T(8,128)(2,1)S(1)}, bf16[64,2048]{1,0:T(8,128)(2,1)S(1)}, u32[]{:S(2)}, u32[]{:S(2)}) collective-permute-start(bf16[64,2048]{1,0:T(8,128)(2,1)S(1)} %get-tuple-element.589), channel_id=1, source_target_pairs={{0,1},{1,2},{2,3},{4,5},{5,6},{6,7},{8,9},{9,10},{10,11},{12,13},{... | collective-permute-start | bytes 786440 | tf_op jit(solution)/shard_map/while/body/eval_jaxpr/ppermute | solution.py:23
  671.0 7.9 all-to-all-start.1
  682.6 24.2 %all-gather.2.cloned.1.call-start = ((), (), s32[]{:S(2)}) async-start(), calls=%async_computation.3 | async-start | bytes 1310720 | tf_op jit(solution)/shard_map/while/body/eval_jaxpr/all_gather | solution.py:134
  740.8 16.4 %collective-permute-start = (bf16[64,2048]{1,0:T(8,128)(2,1)S(1)}, bf16[64,2048]{1,0:T(8,128)(2,1)S(1)}, u32[]{:S(2)}, u32[]{:S(2)}) collective-permute-start(bf16[64,2048]{1,0:T(8,128)(2,1)S(1)} %get-tuple-element.589), channel_id=1, source_target_pairs={{0,1},{1,2},{2,3},{4,5},{5,6},{6,7},{8,9},{9,10},{10,11},{12,13},{... | collective-permute-start | bytes 786440 | tf_op jit(solution)/shard_map/while/body/eval_jaxpr/ppermute | solution.py:23
  757.2 23.8 %all-gather.2.cloned.1.call-start = ((), (), s32[]{:S(2)}) async-start(), calls=%async_computation.3 | async-start | bytes 1310720 | tf_op jit(solution)/shard_map/while/body/eval_jaxpr/all_gather | solution.py:134
  814.9 16.4 %collective-permute-start = (bf16[64,2048]{1,0:T(8,128)(2,1)S(1)}, bf16[64,2048]{1,0:T(8,128)(2,1)S(1)}, u32[]{:S(2)}, u32[]{:S(2)}) collective-permute-start(bf16[64,2048]{1,0:T(8,128)(2,1)S(1)} %get-tuple-element.589), channel_id=1, source_target_pairs={{0,1},{1,2},{2,3},{4,5},{5,6},{6,7},{8,9},{9,10},{10,11},{12,13},{... | collective-permute-start | bytes 786440 | tf_op jit(solution)/shard_map/while/body/eval_jaxpr/ppermute | solution.py:23
  831.3 87.9 %all-reduce.2.cloned.1.call-start = ((), (), s32[]{:S(2)}) async-start(), calls=%async_computation.2 | async-start | bytes 4194304 | tf_op jit(solution)/shard_map/psum | solution.py:28
  (27 other events, 157.2 us)
Sparse Core Ops, SparseCore 0:
  20.5 17.0 all-gather.1
  95.5 16.2 all-gather.1
  169.8 16.2 all-gather.1
  244.5 15.7 all-gather.1
  318.2 16.2 all-gather.1
  392.9 16.2 all-gather.1
  467.1 16.2 all-gather.1
  541.8 16.1 all-gather.1
  615.9 16.3 all-gather.1
  690.6 16.1 all-gather.1
  765.1 15.7 all-gather.1
Sparse Core Ops, SparseCore 1:
  834.2 85.0 all-reduce.1
where the time goes:
time: 932 us; the launch traced here: 928 us
  matrix products  285 us (31%)
  waiting for transfers between devices  231 us (25%)
  blocking collectives  145 us (16%)
  starting transfers between devices  110 us (12%)
  other arithmetic  70.3 us (8%)
  local copies, waits for them, and re-layouts  69.7 us (7%)
  between operations  15.2 us (2%)
    dot_general x11, matrix products, add_outputs(): return jnp.dot(block_cols, w_output, preferred_element_type=jnp.float32)  105 us
    dot_general x11, matrix products, add_columns(): jnp.dot(block_cols, w_query, preferred_element_type=jnp.float32)  96.7 us
    psum x1, waiting for transfers between devices, from_root(): return lax.psum(jnp.where(mine, x, jnp.zeros_like(x)), axis)  86.3 us
    all_gather x11, blocking collectives, one_step(): projected = add_outputs(lax.all_gather(attended, 'tp', axis=1, tiled=True))  78.7 us
    psum x11, blocking collectives, one_step(): mean_sq = lax.psum(partial_sq, 'tp') / MODEL_WIDTH  66.2 us
    all_gather x11, waiting for transfers between devices, one_step(): lax.all_gather(normed, 'tp', axis=1, tiled=True)  61.4 us
    dot_general x11, matrix products, add_columns(): jnp.dot(block_cols, w_keyval, preferred_element_type=jnp.float32)  58.8 us
    all_to_all x11, waiting for transfers between devices, send_pages(): lax.all_to_all(outgoing, 'tp', split_axis=0, concat_axis=0, tiled=True)  47.7 us
  transfers between devices with their start and end apart: 45, of which 34 were waited for; matrix products, arithmetic and copies ran while one was open for 10% of the time, Pallas kernels for 0%

commit v1 on v0

--- a/solution.py
+++ b/solution.py
@@ -11,6 +11,11 @@
 MICRO_BATCHES = 8
 PAGE_TOKENS = 4
 eps_norm = 1e-05
+
+
+def all_parts(x, axis, along):
+    blocks = lax.all_gather(x, axis)
+    return jnp.concatenate(blocks, axis=along)
 
 
 def partner_2(x, axis, apart):
@@ -173,7 +178,7 @@
             "gpqk,kgd->qgpd", weights, kv_view[:, :, 1], preferred_element_type=jnp.float32
         )
         attended = attended.astype(jnp.bfloat16).reshape(row_count, q_heads * head_dim)
-        projected = add_outputs(lax.all_gather(attended, "tp", axis=1, tiled=True))
+        projected = add_outputs(all_parts(attended, "tp", 1))
         produced = (widened + projected).astype(jnp.bfloat16)
         placed = lax.dynamic_update_slice_in_dim(collected, produced, row_start, 0)
         collected = jnp.where(is_live & (section_idx == pp_size - 1), placed, collected)

time: 932 us -> 933 us (level)
  no operation moved by 1% of the time
where the time goes in v1:
time: 933 us; the launch traced here: 929 us
  matrix products  285 us (31%)
  waiting for transfers between devices  231 us (25%)
  blocking collectives  145 us (16%)
  starting transfers between devices  109 us (12%)
  other arithmetic  70.3 us (8%)
  local copies, waits for them, and re-layouts  70.1 us (8%)
  between operations  15.2 us (2%)
    dot_general x11, matrix products, add_outputs(): return jnp.dot(block_cols, w_output, preferred_element_type=jnp.float32)  105 us
    dot_general x11, matrix products, add_columns(): jnp.dot(block_cols, w_query, preferred_element_type=jnp.float32)  96.7 us
    psum x1, waiting for transfers between devices, from_root(): return lax.psum(jnp.where(mine, x, jnp.zeros_like(x)), axis)  86.3 us
    all_gather x11, blocking collectives, all_parts(): blocks = lax.all_gather(x, axis)  78.7 us
    psum x11, blocking collectives, one_step(): mean_sq = lax.psum(partial_sq, 'tp') / MODEL_WIDTH  66.2 us
    all_gather x11, waiting for transfers between devices, one_step(): lax.all_gather(normed, 'tp', axis=1, tiled=True)  61.4 us
    dot_general x11, matrix products, add_columns(): jnp.dot(block_cols, w_keyval, preferred_element_type=jnp.float32)  58.8 us
    all_to_all x11, waiting for transfers between devices, send_pages(): lax.all_to_all(outgoing, 'tp', split_axis=0, concat_axis=0, tiled=True)  47.7 us
  transfers between devices with their start and end apart: 45, of which 34 were waited for; matrix products, arithmetic and copies ran while one was open for 10% of the time, Pallas kernels for 0%

profile of v1, /device:TPU:0, one launch (start us, length us, event | category | flops | bytes accessed | tf_op | source)
XLA Modules:
  0.0 929.0 jit_solution(18335167146415472211)
XLA Ops:
  9.8 822.2 %while.22 = (s32[]{:T(128)}, bf16[64,2048]{1,0:T(8,128)(2,1)S(1)}, bf16[512,512]{1,0:T(8,128)(2,1)S(1)}, bf16[256,4,256]{2,1,0:T(4,128)(2,1)S(1)}, bf16[512,2048...) while((s32[]{:T(128)}, bf16[64,2048]{1,0:T(8,128)(2,1)S(1)}, ...), condition=%wide.region_10.11_spmd.clone, body=%wide.region_0.10_spmd.clone.sunk | while | flops 2923866880 | bytes 67848184 | solution.py:194
  11.1 8.4 psum.24
  43.0 8.8 convolution_convert_fusion.6
  54.5 7.2 all_gather.25
  61.7 9.6 %select_dynamic-update-slice_fusion.2 = (bf16[512,2048]{1,0:T(8,128)(2,1)}, bf16[64,2048]{1,0:T(8,128)(2,1)S(1)}) fusion(bf16[512,2048]{1,0:T(8,128)(2,1)} %get-tuple-element.624, s32[]{:T(128)S(6)} %select_n.328, pred[]{:T(512)S(6)} %and.146, bf16[64,4096]{1,0:T(8,128)(2,1)S(1)} %bitcast.124, bf16[4096,2048]{1,0:T(8,128)(2,1)} %get-tuple-element.658, ...), kind=kOutput, calls=%fused_computation.27.clone.1 | convolution fusion | flops 1074266112 | bytes 18350084 | tf_op jit(solution)/shard_map/while/body/eval_jaxpr/dot_general | solution.py:123
  117.4 8.8 convolution_convert_fusion.6
  129.2 7.2 all_gather.25
  136.4 9.6 %select_dynamic-update-slice_fusion.2 = (bf16[512,2048]{1,0:T(8,128)(2,1)}, bf16[64,2048]{1,0:T(8,128)(2,1)S(1)}) fusion(bf16[512,2048]{1,0:T(8,128)(2,1)} %get-tuple-element.624, s32[]{:T(128)S(6)} %select_n.328, pred[]{:T(512)S(6)} %and.146, bf16[64,4096]{1,0:T(8,128)(2,1)S(1)} %bitcast.124, bf16[4096,2048]{1,0:T(8,128)(2,1)} %get-tuple-element.658, ...), kind=kOutput, calls=%fused_computation.27.clone.1 | convolution fusion | flops 1074266112 | bytes 18350084 | tf_op jit(solution)/shard_map/while/body/eval_jaxpr/dot_general | solution.py:123
  191.7 8.8 convolution_convert_fusion.6
  210.4 9.6 %select_dynamic-update-slice_fusion.2 = (bf16[512,2048]{1,0:T(8,128)(2,1)}, bf16[64,2048]{1,0:T(8,128)(2,1)S(1)}) fusion(bf16[512,2048]{1,0:T(8,128)(2,1)} %get-tuple-element.624, s32[]{:T(128)S(6)} %select_n.328, pred[]{:T(512)S(6)} %and.146, bf16[64,4096]{1,0:T(8,128)(2,1)S(1)} %bitcast.124, bf16[4096,2048]{1,0:T(8,128)(2,1)} %get-tuple-element.658, ...), kind=kOutput, calls=%fused_computation.27.clone.1 | convolution fusion | flops 1074266112 | bytes 18350084 | tf_op jit(solution)/shard_map/while/body/eval_jaxpr/dot_general | solution.py:123
  266.0 8.8 convolution_convert_fusion.6
  277.8 7.2 all_gather.25
  285.0 9.6 %select_dynamic-update-slice_fusion.2 = (bf16[512,2048]{1,0:T(8,128)(2,1)}, bf16[64,2048]{1,0:T(8,128)(2,1)S(1)}) fusion(bf16[512,2048]{1,0:T(8,128)(2,1)} %get-tuple-element.624, s32[]{:T(128)S(6)} %select_n.328, pred[]{:T(512)S(6)} %and.146, bf16[64,4096]{1,0:T(8,128)(2,1)S(1)} %bitcast.124, bf16[4096,2048]{1,0:T(8,128)(2,1)} %get-tuple-element.658, ...), kind=kOutput, calls=%fused_computation.27.clone.1 | convolution fusion | flops 1074266112 | bytes 18350084 | tf_op jit(solution)/shard_map/while/body/eval_jaxpr/dot_general | solution.py:123
  340.3 8.8 convolution_convert_fusion.6
  351.8 7.2 all_gather.25
  358.9 9.6 %select_dynamic-update-slice_fusion.2 = (bf16[512,2048]{1,0:T(8,128)(2,1)}, bf16[64,2048]{1,0:T(8,128)(2,1)S(1)}) fusion(bf16[512,2048]{1,0:T(8,128)(2,1)} %get-tuple-element.624, s32[]{:T(128)S(6)} %select_n.328, pred[]{:T(512)S(6)} %and.146, bf16[64,4096]{1,0:T(8,128)(2,1)S(1)} %bitcast.124, bf16[4096,2048]{1,0:T(8,128)(2,1)} %get-tuple-element.658, ...), kind=kOutput, calls=%fused_computation.27.clone.1 | convolution fusion | flops 1074266112 | bytes 18350084 | tf_op jit(solution)/shard_map/while/body/eval_jaxpr/dot_general | solution.py:123
  415.0 8.8 convolution_convert_fusion.6
  434.1 9.6 %select_dynamic-update-slice_fusion.2 = (bf16[512,2048]{1,0:T(8,128)(2,1)}, bf16[64,2048]{1,0:T(8,128)(2,1)S(1)}) fusion(bf16[512,2048]{1,0:T(8,128)(2,1)} %get-tuple-element.624, s32[]{:T(128)S(6)} %select_n.328, pred[]{:T(512)S(6)} %and.146, bf16[64,4096]{1,0:T(8,128)(2,1)S(1)} %bitcast.124, bf16[4096,2048]{1,0:T(8,128)(2,1)} %get-tuple-element.658, ...), kind=kOutput, calls=%fused_computation.27.clone.1 | convolution fusion | flops 1074266112 | bytes 18350084 | tf_op jit(solution)/shard_map/while/body/eval_jaxpr/dot_general | solution.py:123
  489.3 8.8 convolution_convert_fusion.6
  500.7 7.2 all_gather.25
  507.9 9.6 %select_dynamic-update-slice_fusion.2 = (bf16[512,2048]{1,0:T(8,128)(2,1)}, bf16[64,2048]{1,0:T(8,128)(2,1)S(1)}) fusion(bf16[512,2048]{1,0:T(8,128)(2,1)} %get-tuple-element.624, s32[]{:T(128)S(6)} %select_n.328, pred[]{:T(512)S(6)} %and.146, bf16[64,4096]{1,0:T(8,128)(2,1)S(1)} %bitcast.124, bf16[4096,2048]{1,0:T(8,128)(2,1)} %get-tuple-element.658, ...), kind=kOutput, calls=%fused_computation.27.clone.1 | convolution fusion | flops 1074266112 | bytes 18350084 | tf_op jit(solution)/shard_map/while/body/eval_jaxpr/dot_general | solution.py:123
  563.9 8.8 convolution_convert_fusion.6
  582.9 9.6 %select_dynamic-update-slice_fusion.2 = (bf16[512,2048]{1,0:T(8,128)(2,1)}, bf16[64,2048]{1,0:T(8,128)(2,1)S(1)}) fusion(bf16[512,2048]{1,0:T(8,128)(2,1)} %get-tuple-element.624, s32[]{:T(128)S(6)} %select_n.328, pred[]{:T(512)S(6)} %and.146, bf16[64,4096]{1,0:T(8,128)(2,1)S(1)} %bitcast.124, bf16[4096,2048]{1,0:T(8,128)(2,1)} %get-tuple-element.658, ...), kind=kOutput, calls=%fused_computation.27.clone.1 | convolution fusion | flops 1074266112 | bytes 18350084 | tf_op jit(solution)/shard_map/while/body/eval_jaxpr/dot_general | solution.py:123
  638.2 8.8 convolution_convert_fusion.6
  650.0 7.2 all_gather.25
  657.2 9.6 %select_dynamic-update-slice_fusion.2 = (bf16[512,2048]{1,0:T(8,128)(2,1)}, bf16[64,2048]{1,0:T(8,128)(2,1)S(1)}) fusion(bf16[512,2048]{1,0:T(8,128)(2,1)} %get-tuple-element.624, s32[]{:T(128)S(6)} %select_n.328, pred[]{:T(512)S(6)} %and.146, bf16[64,4096]{1,0:T(8,128)(2,1)S(1)} %bitcast.124, bf16[4096,2048]{1,0:T(8,128)(2,1)} %get-tuple-element.658, ...), kind=kOutput, calls=%fused_computation.27.clone.1 | convolution fusion | flops 1074266112 | bytes 18350084 | tf_op jit(solution)/shard_map/while/body/eval_jaxpr/dot_general | solution.py:123
  712.9 8.8 convolution_convert_fusion.6
  731.9 9.6 %select_dynamic-update-slice_fusion.2 = (bf16[512,2048]{1,0:T(8,128)(2,1)}, bf16[64,2048]{1,0:T(8,128)(2,1)S(1)}) fusion(bf16[512,2048]{1,0:T(8,128)(2,1)} %get-tuple-element.624, s32[]{:T(128)S(6)} %select_n.328, pred[]{:T(512)S(6)} %and.146, bf16[64,4096]{1,0:T(8,128)(2,1)S(1)} %bitcast.124, bf16[4096,2048]{1,0:T(8,128)(2,1)} %get-tuple-element.658, ...), kind=kOutput, calls=%fused_computation.27.clone.1 | convolution fusion | flops 1074266112 | bytes 18350084 | tf_op jit(solution)/shard_map/while/body/eval_jaxpr/dot_general | solution.py:123
  787.1 8.8 convolution_convert_fusion.6
  798.9 7.2 all_gather.25
  806.1 9.6 %select_dynamic-update-slice_fusion.2 = (bf16[512,2048]{1,0:T(8,128)(2,1)}, bf16[64,2048]{1,0:T(8,128)(2,1)S(1)}) fusion(bf16[512,2048]{1,0:T(8,128)(2,1)} %get-tuple-element.624, s32[]{:T(128)S(6)} %select_n.328, pred[]{:T(512)S(6)} %and.146, bf16[64,4096]{1,0:T(8,128)(2,1)S(1)} %bitcast.124, bf16[4096,2048]{1,0:T(8,128)(2,1)} %get-tuple-element.658, ...), kind=kOutput, calls=%fused_computation.27.clone.1 | convolution fusion | flops 1074266112 | bytes 18350084 | tf_op jit(solution)/shard_map/while/body/eval_jaxpr/dot_general | solution.py:123
  833.7 86.3 %all-reduce.2.cloned.1.call-done = bf16[512,2048]{1,0:T(8,128)(2,1)} async-done(((bf16[512,2048]{1,0:T(8,128)(2,1)}), bf16[512,2048]{1,0:T(8,128)(2,1)}) %all-reduce.2.cloned.1.call-update) | async-done | bytes 2097168 | tf_op jit(solution)/shard_map/psum | solution.py:33
  (622 shorter events, 564.1 us)
Async XLA Ops:
  9.8 27.7 %all-gather.2.cloned.1.call-start = ((), (), s32[]{:S(2)}) async-start(), calls=%async_computation.3 | async-start | bytes 1310720 | tf_op jit(solution)/shard_map/while/body/eval_jaxpr/all_gather | solution.py:139
  71.2 16.3 %collective-permute-start = (bf16[64,2048]{1,0:T(8,128)(2,1)S(1)}, bf16[64,2048]{1,0:T(8,128)(2,1)S(1)}, u32[]{:S(2)}, u32[]{:S(2)}) collective-permute-start(bf16[64,2048]{1,0:T(8,128)(2,1)S(1)} %get-tuple-element.589), channel_id=1, source_target_pairs={{0,1},{1,2},{2,3},{4,5},{5,6},{6,7},{8,9},{9,10},{10,11},{12,13},{... | collective-permute-start | bytes 786440 | tf_op jit(solution)/shard_map/while/body/eval_jaxpr/ppermute | solution.py:28
  76.1 7.9 all-to-all-start.1
  87.5 24.3 %all-gather.2.cloned.1.call-start = ((), (), s32[]{:S(2)}) async-start(), calls=%async_computation.3 | async-start | bytes 1310720 | tf_op jit(solution)/shard_map/while/body/eval_jaxpr/all_gather | solution.py:139
  146.0 15.9 %collective-permute-start = (bf16[64,2048]{1,0:T(8,128)(2,1)S(1)}, bf16[64,2048]{1,0:T(8,128)(2,1)S(1)}, u32[]{:S(2)}, u32[]{:S(2)}) collective-permute-start(bf16[64,2048]{1,0:T(8,128)(2,1)S(1)} %get-tuple-element.589), channel_id=1, source_target_pairs={{0,1},{1,2},{2,3},{4,5},{5,6},{6,7},{8,9},{9,10},{10,11},{12,13},{... | collective-permute-start | bytes 786440 | tf_op jit(solution)/shard_map/while/body/eval_jaxpr/ppermute | solution.py:28
  150.4 7.9 all-to-all-start.1
  161.9 24.3 %all-gather.2.cloned.1.call-start = ((), (), s32[]{:S(2)}) async-start(), calls=%async_computation.3 | async-start | bytes 1310720 | tf_op jit(solution)/shard_map/while/body/eval_jaxpr/all_gather | solution.py:139
  219.9 16.7 %collective-permute-start = (bf16[64,2048]{1,0:T(8,128)(2,1)S(1)}, bf16[64,2048]{1,0:T(8,128)(2,1)S(1)}, u32[]{:S(2)}, u32[]{:S(2)}) collective-permute-start(bf16[64,2048]{1,0:T(8,128)(2,1)S(1)} %get-tuple-element.589), channel_id=1, source_target_pairs={{0,1},{1,2},{2,3},{4,5},{5,6},{6,7},{8,9},{9,10},{10,11},{12,13},{... | collective-permute-start | bytes 786440 | tf_op jit(solution)/shard_map/while/body/eval_jaxpr/ppermute | solution.py:28
  225.2 7.9 all-to-all-start.1
  236.7 23.8 %all-gather.2.cloned.1.call-start = ((), (), s32[]{:S(2)}) async-start(), calls=%async_computation.3 | async-start | bytes 1310720 | tf_op jit(solution)/shard_map/while/body/eval_jaxpr/all_gather | solution.py:139
  294.6 15.8 %collective-permute-start = (bf16[64,2048]{1,0:T(8,128)(2,1)S(1)}, bf16[64,2048]{1,0:T(8,128)(2,1)S(1)}, u32[]{:S(2)}, u32[]{:S(2)}) collective-permute-start(bf16[64,2048]{1,0:T(8,128)(2,1)S(1)} %get-tuple-element.589), channel_id=1, source_target_pairs={{0,1},{1,2},{2,3},{4,5},{5,6},{6,7},{8,9},{9,10},{10,11},{12,13},{... | collective-permute-start | bytes 786440 | tf_op jit(solution)/shard_map/while/body/eval_jaxpr/ppermute | solution.py:28
  299.0 7.9 all-to-all-start.1
  310.5 24.3 %all-gather.2.cloned.1.call-start = ((), (), s32[]{:S(2)}) async-start(), calls=%async_computation.3 | async-start | bytes 1310720 | tf_op jit(solution)/shard_map/while/body/eval_jaxpr/all_gather | solution.py:139
  368.5 16.7 %collective-permute-start = (bf16[64,2048]{1,0:T(8,128)(2,1)S(1)}, bf16[64,2048]{1,0:T(8,128)(2,1)S(1)}, u32[]{:S(2)}, u32[]{:S(2)}) collective-permute-start(bf16[64,2048]{1,0:T(8,128)(2,1)S(1)} %get-tuple-element.589), channel_id=1, source_target_pairs={{0,1},{1,2},{2,3},{4,5},{5,6},{6,7},{8,9},{9,10},{10,11},{12,13},{... | collective-permute-start | bytes 786440 | tf_op jit(solution)/shard_map/while/body/eval_jaxpr/ppermute | solution.py:28
  373.8 7.9 all-to-all-start.1
  385.3 24.3 %all-gather.2.cloned.1.call-start = ((), (), s32[]{:S(2)}) async-start(), calls=%async_computation.3 | async-start | bytes 1310720 | tf_op jit(solution)/shard_map/while/body/eval_jaxpr/all_gather | solution.py:139
  443.6 15.9 %collective-permute-start = (bf16[64,2048]{1,0:T(8,128)(2,1)S(1)}, bf16[64,2048]{1,0:T(8,128)(2,1)S(1)}, u32[]{:S(2)}, u32[]{:S(2)}) collective-permute-start(bf16[64,2048]{1,0:T(8,128)(2,1)S(1)} %get-tuple-element.589), channel_id=1, source_target_pairs={{0,1},{1,2},{2,3},{4,5},{5,6},{6,7},{8,9},{9,10},{10,11},{12,13},{... | collective-permute-start | bytes 786440 | tf_op jit(solution)/shard_map/while/body/eval_jaxpr/ppermute | solution.py:28
  448.1 7.9 all-to-all-start.1
  459.5 24.2 %all-gather.2.cloned.1.call-start = ((), (), s32[]{:S(2)}) async-start(), calls=%async_computation.3 | async-start | bytes 1310720 | tf_op jit(solution)/shard_map/while/body/eval_jaxpr/all_gather | solution.py:139
  517.4 16.8 %collective-permute-start = (bf16[64,2048]{1,0:T(8,128)(2,1)S(1)}, bf16[64,2048]{1,0:T(8,128)(2,1)S(1)}, u32[]{:S(2)}, u32[]{:S(2)}) collective-permute-start(bf16[64,2048]{1,0:T(8,128)(2,1)S(1)} %get-tuple-element.589), channel_id=1, source_target_pairs={{0,1},{1,2},{2,3},{4,5},{5,6},{6,7},{8,9},{9,10},{10,11},{12,13},{... | collective-permute-start | bytes 786440 | tf_op jit(solution)/shard_map/while/body/eval_jaxpr/ppermute | solution.py:28
  522.8 7.9 all-to-all-start.1
  534.2 24.2 %all-gather.2.cloned.1.call-start = ((), (), s32[]{:S(2)}) async-start(), calls=%async_computation.3 | async-start | bytes 1310720 | tf_op jit(solution)/shard_map/while/body/eval_jaxpr/all_gather | solution.py:139
  592.5 15.9 %collective-permute-start = (bf16[64,2048]{1,0:T(8,128)(2,1)S(1)}, bf16[64,2048]{1,0:T(8,128)(2,1)S(1)}, u32[]{:S(2)}, u32[]{:S(2)}) collective-permute-start(bf16[64,2048]{1,0:T(8,128)(2,1)S(1)} %get-tuple-element.589), channel_id=1, source_target_pairs={{0,1},{1,2},{2,3},{4,5},{5,6},{6,7},{8,9},{9,10},{10,11},{12,13},{... | collective-permute-start | bytes 786440 | tf_op jit(solution)/shard_map/while/body/eval_jaxpr/ppermute | solution.py:28
  596.9 7.9 all-to-all-start.1
  608.4 24.3 %all-gather.2.cloned.1.call-start = ((), (), s32[]{:S(2)}) async-start(), calls=%async_computation.3 | async-start | bytes 1310720 | tf_op jit(solution)/shard_map/while/body/eval_jaxpr/all_gather | solution.py:139
  666.8 16.4 %collective-permute-start = (bf16[64,2048]{1,0:T(8,128)(2,1)S(1)}, bf16[64,2048]{1,0:T(8,128)(2,1)S(1)}, u32[]{:S(2)}, u32[]{:S(2)}) collective-permute-start(bf16[64,2048]{1,0:T(8,128)(2,1)S(1)} %get-tuple-element.589), channel_id=1, source_target_pairs={{0,1},{1,2},{2,3},{4,5},{5,6},{6,7},{8,9},{9,10},{10,11},{12,13},{... | collective-permute-start | bytes 786440 | tf_op jit(solution)/shard_map/while/body/eval_jaxpr/ppermute | solution.py:28
  671.7 7.9 all-to-all-start.1
  683.2 24.2 %all-gather.2.cloned.1.call-start = ((), (), s32[]{:S(2)}) async-start(), calls=%async_computation.3 | async-start | bytes 1310720 | tf_op jit(solution)/shard_map/while/body/eval_jaxpr/all_gather | solution.py:139
  741.4 16.4 %collective-permute-start = (bf16[64,2048]{1,0:T(8,128)(2,1)S(1)}, bf16[64,2048]{1,0:T(8,128)(2,1)S(1)}, u32[]{:S(2)}, u32[]{:S(2)}) collective-permute-start(bf16[64,2048]{1,0:T(8,128)(2,1)S(1)} %get-tuple-element.589), channel_id=1, source_target_pairs={{0,1},{1,2},{2,3},{4,5},{5,6},{6,7},{8,9},{9,10},{10,11},{12,13},{... | collective-permute-start | bytes 786440 | tf_op jit(solution)/shard_map/while/body/eval_jaxpr/ppermute | solution.py:28
  757.8 23.8 %all-gather.2.cloned.1.call-start = ((), (), s32[]{:S(2)}) async-start(), calls=%async_computation.3 | async-start | bytes 1310720 | tf_op jit(solution)/shard_map/while/body/eval_jaxpr/all_gather | solution.py:139
  815.7 16.4 %collective-permute-start = (bf16[64,2048]{1,0:T(8,128)(2,1)S(1)}, bf16[64,2048]{1,0:T(8,128)(2,1)S(1)}, u32[]{:S(2)}, u32[]{:S(2)}) collective-permute-start(bf16[64,2048]{1,0:T(8,128)(2,1)S(1)} %get-tuple-element.589), channel_id=1, source_target_pairs={{0,1},{1,2},{2,3},{4,5},{5,6},{6,7},{8,9},{9,10},{10,11},{12,13},{... | collective-permute-start | bytes 786440 | tf_op jit(solution)/shard_map/while/body/eval_jaxpr/ppermute | solution.py:28
  832.1 87.9 %all-reduce.2.cloned.1.call-start = ((), (), s32[]{:S(2)}) async-start(), calls=%async_computation.2 | async-start | bytes 4194304 | tf_op jit(solution)/shard_map/psum | solution.py:33
  (27 other events, 157.2 us)
Sparse Core Ops, SparseCore 0:
  20.5 17.0 all-gather.1
  95.6 16.2 all-gather.1
  169.9 16.2 all-gather.1
  244.7 15.7 all-gather.1
  318.5 16.2 all-gather.1
  393.2 16.2 all-gather.1
  467.5 16.2 all-gather.1
  542.3 16.1 all-gather.1
  616.4 16.3 all-gather.1
  691.2 16.1 all-gather.1
  765.8 15.7 all-gather.1
Sparse Core Ops, SparseCore 1:
  834.9 85.0 all-reduce.1
